TPU v7x, 32 devices: a whole 2x2x4 slice. The times are simulated.
32 devices in a mesh: gx: 8 (over y, x, core), gy: 4 (over z).
Axes of the slice: x: 2, y: 2, z: 4, core: 2. Of those that a mesh axis runs over, the one named last changes fastest.
Arguments:
- candidate_owner: int32 [256, 512, 1], P(('gx', 'gy')), may hold values from 0 to 31; in each aligned block of 4096 rows (0 to 4095, 4096 to 8191, ..., all dimensions but the last counted through in order) at most 256 rows name the same one
- candidate_row: int32 [256, 512], P(('gx', 'gy')), may hold values from 0 to 78335
- item_table: bfloat16 [2506752, 128], P(('gx', 'gy')), may hold values from -6 to 6
- w_in: bfloat16 [128, 512], replicated, may hold values from -0.5 to 0.5
- w_qkv: bfloat16 [1, 512, 1536], replicated, may hold values from -0.25 to 0.25
- w_out: bfloat16 [1, 512, 512], replicated, may hold values from -0.25 to 0.25
- w_up: bfloat16 [1, 512, 1024], replicated, may hold values from -0.25 to 0.25
- w_down: bfloat16 [1, 1024, 512], replicated, may hold values from -0.1875 to 0.1875
- norm_gains: float32 [1, 2, 512], replicated, may hold values from 0.25 to 1.75
- final_gain: float32 [512], replicated, may hold values from 0.25 to 1.75
- w_score: bfloat16 [512], replicated, may hold values from -0.25 to 0.25
Outputs:
- log_probs: float32 [256, 512], P(('gx', 'gy'))
Inputs may be any that keep to these rules, and one draw needn't show every extreme that they name: `candidate_owner`: among the candidates of one device's 8 slates no shard is named more than 256 times, a bound that some block reaches.
All inputs are finite; a program needn't handle non-finite values.
Results may differ from a plain program's by a relative error of at most 0.0007.
Values may be sent and summed in bfloat16 or wider, within the bound.
A program may use at most 128 MiB of HBM per device.

v0:
```python
import jax
import jax.numpy as jnp
from jax import lax
from jax.sharding import PartitionSpec as P

HEADS = 8


def layer_norm(values, gain):
    mean = jnp.mean(values, axis=-1, keepdims=True)
    centred = values - mean
    variance = jnp.mean(centred * centred, axis=-1, keepdims=True)
    return centred * lax.rsqrt(variance + 1e-05) * gain


def attend_slate(operands):
    query, keys, values = operands
    length = query.shape[0]
    head_dim = query.shape[-1]
    scores = jnp.einsum(
        "qhd,khd->hqk", query, keys, preferred_element_type=jnp.float32
    ) * head_dim ** (-0.5)
    probs = jax.nn.softmax(scores, axis=-1).astype(jnp.bfloat16)
    mixed = jnp.einsum("hqk,khd->qhd", probs, values, preferred_element_type=jnp.float32)
    return mixed.astype(jnp.bfloat16).reshape(length, HEADS * head_dim)


def score_slates(emb, w_in, w_qkv, w_out, w_up, w_down, norm_gains, final_gain, w_score):
    slates, length, width = emb.shape
    model = w_in.shape[1]
    head_dim = model // HEADS
    resid = jnp.dot(emb.reshape(slates * length, width), w_in, preferred_element_type=jnp.float32)
    normed = layer_norm(resid, norm_gains[0, 0]).astype(jnp.bfloat16)
    weights = w_qkv[0]
    query = jnp.dot(normed, weights[:, :model], preferred_element_type=jnp.float32).astype(
        jnp.bfloat16
    )
    keys = jnp.dot(
        normed, weights[:, model : 2 * model], preferred_element_type=jnp.float32
    ).astype(jnp.bfloat16)
    values = jnp.dot(normed, weights[:, 2 * model :], preferred_element_type=jnp.float32).astype(
        jnp.bfloat16
    )
    query = query.reshape(slates, length, HEADS, head_dim)
    keys = keys.reshape(slates, length, HEADS, head_dim)
    values = values.reshape(slates, length, HEADS, head_dim)
    mixed = lax.map(attend_slate, (query, keys, values)).reshape(slates * length, model)
    resid = resid + jnp.dot(mixed, w_out[0], preferred_element_type=jnp.float32)
    normed = layer_norm(resid, norm_gains[0, 1]).astype(jnp.bfloat16)
    inner = jax.nn.gelu(jnp.dot(normed, w_up[0], preferred_element_type=jnp.float32)).astype(
        jnp.bfloat16
    )
    resid = resid + jnp.dot(inner, w_down[0], preferred_element_type=jnp.float32)
    final = layer_norm(resid, final_gain)
    logits = jnp.sum(final * w_score.astype(jnp.float32)[None, :], axis=-1)
    return jax.nn.log_softmax(logits.reshape(slates, length), axis=-1)


def slot_numbers(owner, shards, length):
    total = owner.shape[0]
    onehot = (owner[:, None] == jnp.arange(shards, dtype=jnp.int32)[None, :]).astype(jnp.bfloat16)
    blocks = onehot.reshape(total // length, length, shards)
    lower = (jnp.arange(length)[:, None] >= jnp.arange(length)[None, :]).astype(jnp.bfloat16)
    within = jnp.einsum("ij,bjn->bin", lower, blocks, preferred_element_type=jnp.float32)
    totals = within[:, -1, :]
    before = jnp.cumsum(totals, axis=0) - totals
    counts = within + before[:, None, :]
    picked = jnp.sum(counts * blocks.astype(jnp.float32), axis=-1)
    return (picked.reshape(total) - 1.0).astype(jnp.int32)


def fetch_rows(item_table, wanted):
    flat = wanted.reshape(-1)
    rows = jnp.take(item_table, jnp.maximum(flat, 0), axis=0)
    rows = jnp.where((flat >= 0)[:, None], rows, jnp.zeros_like(rows))
    return rows.reshape(wanted.shape + (item_table.shape[1],))


def per_device(
    candidate_owner,
    candidate_row,
    item_table,
    w_in,
    w_qkv,
    w_out,
    w_up,
    w_down,
    norm_gains,
    final_gain,
    w_score,
):
    slates, length, unused = candidate_owner.shape
    width = item_table.shape[1]
    shards = lax.axis_size(("gx", "gy"))
    capacity = max(2, 2 * slates * length // shards)
    owner = candidate_owner.reshape(slates * length)
    row_index = candidate_row.reshape(slates * length)
    slot = slot_numbers(owner, shards, length)
    position = owner * capacity + slot
    outgoing = jnp.full((shards * capacity,), -1, jnp.int32).at[position].set(row_index)
    outgoing = outgoing.reshape(shards, capacity)
    found = fetch_rows(
        item_table, lax.all_to_all(outgoing, ("gx", "gy"), split_axis=0, concat_axis=0, tiled=True)
    )
    returned = lax.all_to_all(found, ("gx", "gy"), split_axis=0, concat_axis=0, tiled=True)
    returned = returned.reshape(shards * capacity, width)
    emb = jnp.take(returned, position, axis=0).reshape(slates, length, width)
    return score_slates(emb, w_in, w_qkv, w_out, w_up, w_down, norm_gains, final_gain, w_score)


def solution(mesh):
    return jax.shard_map(
        per_device,
        mesh=mesh,
        in_specs=(
            P(("gx", "gy"), None, None),
            P(("gx", "gy"), None),
            P(("gx", "gy"), None),
            P(),
            P(),
            P(),
            P(),
            P(),
            P(),
            P(),
            P(),
        ),
        out_specs=P(("gx", "gy"), None),
        check_vma=False,
    )
```

profile of v0, /device:TPU:1, one launch (start us, length us, event | category | flops | bytes accessed | tf_op | source)
XLA Modules:
  0.0 355.7 jit_solution(8072462239938948020)
XLA Ops:
  3.1 15.5 %scatter_custom_fusion = s32[8192]{0:T(1024)S(1)} fusion(s32[4096]{0:T(1024)S(1)} %bitcast.103, s32[4096]{0:T(1024)S(1)} %bitcast.110, s32[]{:T(128)} %constant.82.clone.1), kind=kCustom, calls=%fused_computation.85 | custom fusion | bytes 32772 | tf_op jit(solution)/shard_map/scatter | solution.py:100
  18.7 13.7 %all_to_all.14 = s32[32,1,256]{2,1,0:T(1,128)S(1)} all-to-all(s32[32,1,256]{2,1,0:T(1,128)S(1)} %bitcast.101), channel_id=1, replica_groups=mesh['gx'=8,'gy'=4] {'gx','gy'}, dimensions={0} | all-to-all | bytes 65536 | tf_op jit(solution)/shard_map/all_to_all | solution.py:103
  32.4 31.2 %gather_fusion = bf16[8192,128]{1,0:T(8,128)(2,1)S(1)} fusion(bf16[78336,128]{1,0:T(8,128)(2,1)} %param.15, s32[8192]{0:T(1024)S(1)} %broadcast_clamp_fusion), kind=kCustom, calls=%fused_computation | custom fusion | bytes 4227072 | tf_op jit(solution)/shard_map/jit(_take)/gather | solution.py:74
  63.6 4.6 %select_select_fusion = bf16[32,256,128]{2,1,0:T(8,128)(2,1)} fusion(bf16[32,256,128]{2,1,0:T(8,128)(2,1)S(1)} %bitcast.98, pred[32,256]{1,0:T(8,128)(4,1)S(1)} %get-tuple-element.66, pred[32,256]{1,0:T(8,128)(4,1)S(1)} %get-tuple-element.65), kind=kLoop, calls=%fused_computation.53 | loop fusion | flops 2097152 | bytes 4210688 | tf_op jit(solution)/shard_map/jit(_where)/select_n | solution.py:75
  68.2 3.1 all-to-all-start.1
  71.9 47.8 %all-to-all-done.1 = bf16[32,256,128]{2,1,0:T(8,128)(2,1)S(1)} async-done(((bf16[32,256,128]{2,1,0:T(8,128)(2,1)}), bf16[32,256,128]{2,1,0:T(8,128)(2,1)S(1)}, u32[]{:S(2)}, u32[]{:S(2)}) %all-to-all-start.1) | async-done | bytes 2097184 | tf_op jit(solution)/shard_map/all_to_all | solution.py:105
  119.7 14.9 %gather_fusion.1 = bf16[4096,128]{1,0:T(8,128)(2,1)} fusion(bf16[8192,128]{1,0:T(8,128)(2,1)S(1)} %bitcast.95, s32[4096]{0:T(1024)S(1)} %broadcast_clamp_fusion.1), kind=kCustom, calls=%fused_computation.1 | custom fusion | bytes 2113536 | tf_op jit(solution)/shard_map/jit(_take)/gather | solution.py:107
  134.6 3.7 %fusion.92 = (f32[4096]{0:T(1024)S(1)}, f32[4096,512]{0,1:T(8,128)S(1)}) fusion(bf16[128,512]{1,0:T(8,128)(2,1)S(1)} %copy-done.5, bf16[4096,128]{1,0:T(8,128)(2,1)} %gather_fusion.1, pred[4096]{0:T(1024)(128)(4,1)S(1)} %compare_and_fusion), kind=kOutput, calls=%fused_computation.104 | convolution fusion | flops 539488256 | bytes 9588736 | tf_op jit(solution)/shard_map/dot_general | solution.py:32
  138.3 1.0 multiply_reduce_fusion.4
  139.4 1.5 multiply_convert_fusion.1
  141.9 4.4 %convolution_convert_fusion.2 = bf16[4096,512]{1,0:T(8,128)(2,1)} fusion(bf16[4096,512]{0,1:T(8,128)(2,1)S(1)} %multiply_convert_fusion.1, bf16[512,1536]{1,0:T(8,128)(2,1)S(1)} %bitcast.113), kind=kOutput, calls=%fused_computation.48 | convolution fusion | flops 2149580800 | bytes 8912896 | tf_op jit(solution)/shard_map/dot_general | solution.py:41
  146.3 4.4 %convolution_convert_fusion.1 = bf16[4096,512]{1,0:T(8,128)(2,1)} fusion(bf16[4096,512]{0,1:T(8,128)(2,1)S(1)} %multiply_convert_fusion.1, bf16[512,1536]{1,0:T(8,128)(2,1)S(1)} %bitcast.114), kind=kOutput, calls=%fused_computation.47 | convolution fusion | flops 2149580800 | bytes 8912896 | tf_op jit(solution)/shard_map/dot_general | solution.py:35
  150.7 4.4 %convolution_convert_fusion = bf16[4096,512]{1,0:T(8,128)(2,1)} fusion(bf16[4096,512]{0,1:T(8,128)(2,1)S(1)} %multiply_convert_fusion.1, bf16[512,1536]{1,0:T(8,128)(2,1)S(1)} %bitcast.115), kind=kOutput, calls=%fused_computation.46 | convolution fusion | flops 2149580800 | bytes 8912896 | tf_op jit(solution)/shard_map/dot_general | solution.py:38
  155.2 11.2 %reshape.228 = bf16[8,512,8,64]{3,2,1,0:T(8,128)(2,1)} reshape(bf16[4096,512]{1,0:T(8,128)(2,1)} %convolution_convert_fusion.2) | data formatting | bytes 8388608 | tf_op jit(solution)/shard_map/reshape | solution.py:46
  166.4 9.8 %copy.38 = bf16[8,512,8,64]{1,3,2,0:T(8,128)(2,1)} copy(bf16[8,512,8,64]{3,2,1,0:T(8,128)(2,1)} %reshape.228) | data formatting | bytes 8388608 | tf_op jit(solution)/shard_map/while | solution.py:47
  176.1 11.2 %reshape.229 = bf16[8,512,8,64]{3,2,1,0:T(8,128)(2,1)} reshape(bf16[4096,512]{1,0:T(8,128)(2,1)} %convolution_convert_fusion.1) | data formatting | bytes 8388608 | tf_op jit(solution)/shard_map/reshape | solution.py:44
  187.3 9.7 %copy.39 = bf16[8,512,8,64]{1,3,2,0:T(8,128)(2,1)} copy(bf16[8,512,8,64]{3,2,1,0:T(8,128)(2,1)} %reshape.229) | data formatting | bytes 8388608 | tf_op jit(solution)/shard_map/while | solution.py:47
  197.1 11.2 %reshape.230 = bf16[8,512,8,64]{3,2,1,0:T(8,128)(2,1)} reshape(bf16[4096,512]{1,0:T(8,128)(2,1)} %convolution_convert_fusion) | data formatting | bytes 8388608 | tf_op jit(solution)/shard_map/reshape | solution.py:45
  208.3 9.7 %copy.40 = bf16[8,512,8,64]{1,3,2,0:T(8,128)(2,1)} copy(bf16[8,512,8,64]{3,2,1,0:T(8,128)(2,1)} %reshape.230) | data formatting | bytes 8388608 | tf_op jit(solution)/shard_map/while | solution.py:47
  218.0 101.8 %while.10 = (s32[]{:T(128)}, bf16[8,512,512]{2,1,0:T(8,128)(2,1)}, bf16[8,512,8,64]{1,3,2,0:T(8,128)(2,1)}, bf16[8,512,8,64]{1,3,2,0:T(8,128)(2,1)}, bf16[8,512,8,64]{1,3,2,0:T(8,128)(2,1)}, /*index=5*/s32[]{:T(128)}) while((s32[]{:T(128)}, bf16[8,512,512]{2,1,0:T(8,128)(2,1)}, bf16[8,512,8,64]{1,3,2,0:T(8,128)(2,1)}, ...), condition=%wide.region_8.9_spmd, body=%wide.region_5.8_spmd.sunk | while | flops 547619328 | bytes 21006404 | solution.py:47
  218.0 7.3 %fusion.110 = (f32[8,512]{1,0:T(8,128)S(1)}, f32[8,512,512]{1,2,0:T(8,128)}) fusion(bf16[8,512,8,64]{1,3,2,0:T(8,128)(2,1)} %get-tuple-element.128, s32[]{:T(128)} %get-tuple-element.118, bf16[8,512,8,64]{1,3,2,0:T(8,128)(2,1)} %get-tuple-element.127), kind=kOutput, calls=%fused_computation.101.clone.1 | convolution fusion | flops 274727424 | bytes 9454592 | tf_op jit(solution)/shard_map/while/body/eval_jaxpr/sub | solution.py:23
  225.3 4.4 %fusion.111 = bf16[8,64,512]{2,1,0:T(8,128)(2,1)S(1)} fusion(f32[8,512,512]{1,2,0:T(8,128)} %get-tuple-element.110, f32[8,512]{1,0:T(8,128)S(1)} %get-tuple-element.111, bf16[8,512,8,64]{1,3,2,0:T(8,128)(2,1)} %get-tuple-element.126, s32[]{:T(128)} %get-tuple-element.118), kind=kOutput, calls=%fused_computation.10.clone.1 | convolution fusion | flops 272891904 | bytes 9454080 | tf_op jit(solution)/shard_map/while/body/eval_jaxpr/hqk,khd->qhd/dot_general | solution.py:24
  229.9 0.9 constant_dynamic-update-slice_fusion.2
  230.8 7.2 %fusion.110 = (f32[8,512]{1,0:T(8,128)S(1)}, f32[8,512,512]{1,2,0:T(8,128)}) fusion(bf16[8,512,8,64]{1,3,2,0:T(8,128)(2,1)} %get-tuple-element.128, s32[]{:T(128)} %get-tuple-element.118, bf16[8,512,8,64]{1,3,2,0:T(8,128)(2,1)} %get-tuple-element.127), kind=kOutput, calls=%fused_computation.101.clone.1 | convolution fusion | flops 274727424 | bytes 9454592 | tf_op jit(solution)/shard_map/while/body/eval_jaxpr/sub | solution.py:23
  238.0 4.4 %fusion.111 = bf16[8,64,512]{2,1,0:T(8,128)(2,1)S(1)} fusion(f32[8,512,512]{1,2,0:T(8,128)} %get-tuple-element.110, f32[8,512]{1,0:T(8,128)S(1)} %get-tuple-element.111, bf16[8,512,8,64]{1,3,2,0:T(8,128)(2,1)} %get-tuple-element.126, s32[]{:T(128)} %get-tuple-element.118), kind=kOutput, calls=%fused_computation.10.clone.1 | convolution fusion | flops 272891904 | bytes 9454080 | tf_op jit(solution)/shard_map/while/body/eval_jaxpr/hqk,khd->qhd/dot_general | solution.py:24
  242.7 0.9 constant_dynamic-update-slice_fusion.2
  243.6 7.2 %fusion.110 = (f32[8,512]{1,0:T(8,128)S(1)}, f32[8,512,512]{1,2,0:T(8,128)}) fusion(bf16[8,512,8,64]{1,3,2,0:T(8,128)(2,1)} %get-tuple-element.128, s32[]{:T(128)} %get-tuple-element.118, bf16[8,512,8,64]{1,3,2,0:T(8,128)(2,1)} %get-tuple-element.127), kind=kOutput, calls=%fused_computation.101.clone.1 | convolution fusion | flops 274727424 | bytes 9454592 | tf_op jit(solution)/shard_map/while/body/eval_jaxpr/sub | solution.py:23
  250.8 4.4 %fusion.111 = bf16[8,64,512]{2,1,0:T(8,128)(2,1)S(1)} fusion(f32[8,512,512]{1,2,0:T(8,128)} %get-tuple-element.110, f32[8,512]{1,0:T(8,128)S(1)} %get-tuple-element.111, bf16[8,512,8,64]{1,3,2,0:T(8,128)(2,1)} %get-tuple-element.126, s32[]{:T(128)} %get-tuple-element.118), kind=kOutput, calls=%fused_computation.10.clone.1 | convolution fusion | flops 272891904 | bytes 9454080 | tf_op jit(solution)/shard_map/while/body/eval_jaxpr/hqk,khd->qhd/dot_general | solution.py:24
  256.3 7.2 %fusion.110 = (f32[8,512]{1,0:T(8,128)S(1)}, f32[8,512,512]{1,2,0:T(8,128)}) fusion(bf16[8,512,8,64]{1,3,2,0:T(8,128)(2,1)} %get-tuple-element.128, s32[]{:T(128)} %get-tuple-element.118, bf16[8,512,8,64]{1,3,2,0:T(8,128)(2,1)} %get-tuple-element.127), kind=kOutput, calls=%fused_computation.101.clone.1 | convolution fusion | flops 274727424 | bytes 9454592 | tf_op jit(solution)/shard_map/while/body/eval_jaxpr/sub | solution.py:23
  263.5 4.4 %fusion.111 = bf16[8,64,512]{2,1,0:T(8,128)(2,1)S(1)} fusion(f32[8,512,512]{1,2,0:T(8,128)} %get-tuple-element.110, f32[8,512]{1,0:T(8,128)S(1)} %get-tuple-element.111, bf16[8,512,8,64]{1,3,2,0:T(8,128)(2,1)} %get-tuple-element.126, s32[]{:T(128)} %get-tuple-element.118), kind=kOutput, calls=%fused_computation.10.clone.1 | convolution fusion | flops 272891904 | bytes 9454080 | tf_op jit(solution)/shard_map/while/body/eval_jaxpr/hqk,khd->qhd/dot_general | solution.py:24
  269.0 7.2 %fusion.110 = (f32[8,512]{1,0:T(8,128)S(1)}, f32[8,512,512]{1,2,0:T(8,128)}) fusion(bf16[8,512,8,64]{1,3,2,0:T(8,128)(2,1)} %get-tuple-element.128, s32[]{:T(128)} %get-tuple-element.118, bf16[8,512,8,64]{1,3,2,0:T(8,128)(2,1)} %get-tuple-element.127), kind=kOutput, calls=%fused_computation.101.clone.1 | convolution fusion | flops 274727424 | bytes 9454592 | tf_op jit(solution)/shard_map/while/body/eval_jaxpr/sub | solution.py:23
  276.2 4.4 %fusion.111 = bf16[8,64,512]{2,1,0:T(8,128)(2,1)S(1)} fusion(f32[8,512,512]{1,2,0:T(8,128)} %get-tuple-element.110, f32[8,512]{1,0:T(8,128)S(1)} %get-tuple-element.111, bf16[8,512,8,64]{1,3,2,0:T(8,128)(2,1)} %get-tuple-element.126, s32[]{:T(128)} %get-tuple-element.118), kind=kOutput, calls=%fused_computation.10.clone.1 | convolution fusion | flops 272891904 | bytes 9454080 | tf_op jit(solution)/shard_map/while/body/eval_jaxpr/hqk,khd->qhd/dot_general | solution.py:24
  280.8 0.9 constant_dynamic-update-slice_fusion.2
  281.7 7.2 %fusion.110 = (f32[8,512]{1,0:T(8,128)S(1)}, f32[8,512,512]{1,2,0:T(8,128)}) fusion(bf16[8,512,8,64]{1,3,2,0:T(8,128)(2,1)} %get-tuple-element.128, s32[]{:T(128)} %get-tuple-element.118, bf16[8,512,8,64]{1,3,2,0:T(8,128)(2,1)} %get-tuple-element.127), kind=kOutput, calls=%fused_computation.101.clone.1 | convolution fusion | flops 274727424 | bytes 9454592 | tf_op jit(solution)/shard_map/while/body/eval_jaxpr/sub | solution.py:23
  288.9 4.4 %fusion.111 = bf16[8,64,512]{2,1,0:T(8,128)(2,1)S(1)} fusion(f32[8,512,512]{1,2,0:T(8,128)} %get-tuple-element.110, f32[8,512]{1,0:T(8,128)S(1)} %get-tuple-element.111, bf16[8,512,8,64]{1,3,2,0:T(8,128)(2,1)} %get-tuple-element.126, s32[]{:T(128)} %get-tuple-element.118), kind=kOutput, calls=%fused_computation.10.clone.1 | convolution fusion | flops 272891904 | bytes 9454080 | tf_op jit(solution)/shard_map/while/body/eval_jaxpr/hqk,khd->qhd/dot_general | solution.py:24
  293.6 0.9 constant_dynamic-update-slice_fusion.2
  294.4 7.2 %fusion.110 = (f32[8,512]{1,0:T(8,128)S(1)}, f32[8,512,512]{1,2,0:T(8,128)}) fusion(bf16[8,512,8,64]{1,3,2,0:T(8,128)(2,1)} %get-tuple-element.128, s32[]{:T(128)} %get-tuple-element.118, bf16[8,512,8,64]{1,3,2,0:T(8,128)(2,1)} %get-tuple-element.127), kind=kOutput, calls=%fused_computation.101.clone.1 | convolution fusion | flops 274727424 | bytes 9454592 | tf_op jit(solution)/shard_map/while/body/eval_jaxpr/sub | solution.py:23
  301.6 4.4 %fusion.111 = bf16[8,64,512]{2,1,0:T(8,128)(2,1)S(1)} fusion(f32[8,512,512]{1,2,0:T(8,128)} %get-tuple-element.110, f32[8,512]{1,0:T(8,128)S(1)} %get-tuple-element.111, bf16[8,512,8,64]{1,3,2,0:T(8,128)(2,1)} %get-tuple-element.126, s32[]{:T(128)} %get-tuple-element.118), kind=kOutput, calls=%fused_computation.10.clone.1 | convolution fusion | flops 272891904 | bytes 9454080 | tf_op jit(solution)/shard_map/while/body/eval_jaxpr/hqk,khd->qhd/dot_general | solution.py:24
  307.1 7.2 %fusion.110 = (f32[8,512]{1,0:T(8,128)S(1)}, f32[8,512,512]{1,2,0:T(8,128)}) fusion(bf16[8,512,8,64]{1,3,2,0:T(8,128)(2,1)} %get-tuple-element.128, s32[]{:T(128)} %get-tuple-element.118, bf16[8,512,8,64]{1,3,2,0:T(8,128)(2,1)} %get-tuple-element.127), kind=kOutput, calls=%fused_computation.101.clone.1 | convolution fusion | flops 274727424 | bytes 9454592 | tf_op jit(solution)/shard_map/while/body/eval_jaxpr/sub | solution.py:23
  314.3 4.4 %fusion.111 = bf16[8,64,512]{2,1,0:T(8,128)(2,1)S(1)} fusion(f32[8,512,512]{1,2,0:T(8,128)} %get-tuple-element.110, f32[8,512]{1,0:T(8,128)S(1)} %get-tuple-element.111, bf16[8,512,8,64]{1,3,2,0:T(8,128)(2,1)} %get-tuple-element.126, s32[]{:T(128)} %get-tuple-element.118), kind=kOutput, calls=%fused_computation.10.clone.1 | convolution fusion | flops 272891904 | bytes 9454080 | tf_op jit(solution)/shard_map/while/body/eval_jaxpr/hqk,khd->qhd/dot_general | solution.py:24
  319.0 0.8 constant_dynamic-update-slice_fusion.2
  319.8 7.1 %fusion.93 = (f32[4096]{0:T(1024)S(1)}, f32[4096,512]{0,1:T(8,128)S(1)}) fusion(f32[4096,512]{0,1:T(8,128)} %copy-done.1, bf16[4096,512]{1,0:T(8,128)(2,1)} %bitcast.97, bf16[1,512,512]{2,1,0:T(8,128)(2,1)S(1)} %copy-done.4), kind=kOutput, calls=%fused_computation.105 | convolution fusion | flops 2151673856 | bytes 21512192 | tf_op jit(solution)/shard_map/dot_general | solution.py:48
  327.0 3.2 copy-done.2
  330.1 1.0 multiply_reduce_fusion.3
  331.2 15.8 %fusion.94 = (f32[4096]{0:T(1024)S(1)}, f32[4096,512]{0,1:T(8,128)}) fusion(f32[4096,512]{0,1:T(8,128)} %copy-done.2, bf16[1,1024,512]{2,1,0:T(8,128)(2,1)S(1)} %copy-done, f32[512]{0:T(512)S(1)} %bitcast.112, f32[4096]{0:T(1024)S(1)} %add_rsqrt_fusion.1, f32[4096]{0:T(1024)S(1)} %broadcast_multiply_fusion.1, bf16[1,512,1024]{2,1,0:T(8,128)(2,1)S(1)} %copy-done.11), kind=kOutput, calls=%fused_computation.106 | convolution fusion | flops 8640262144 | bytes 18925568 | tf_op jit(solution)/shard_map/dot_general | solution.py:53
  347.0 4.5 %multiply_reduce_fusion.2 = f32[4096]{0:T(1024)S(1)} fusion(f32[4096,512]{0,1:T(8,128)} %get-tuple-element.76, f32[4096]{0:T(1024)S(1)} %broadcast_multiply_fusion), kind=kLoop, calls=%fused_computation.38 | loop fusion | flops 6287360 | bytes 8421376 | tf_op jit(solution)/shard_map/reduce_sum | solution.py:12
  351.5 1.2 copy-done.3
  352.7 2.0 multiply_reduce_fusion.1
  (63 shorter events, 10.0 us)
Async XLA Ops:
  0.0 331.2 %copy-start = (bf16[1,1024,512]{2,1,0:T(8,128)(2,1)S(1)}, bf16[1,1024,512]{2,1,0:T(8,128)(2,1)}, u32[]{:S(2)}) copy-start(bf16[1,1024,512]{2,1,0:T(8,128)(2,1)} %param.20) | copy-start | bytes 3145732
  63.5 7.8 %copy-start.9 = (bf16[512]{0:T(512)(128)(2,1)S(1)}, bf16[512]{0:T(512)(128)(2,1)}, u32[]{:S(2)}) copy-start(bf16[512]{0:T(512)(128)(2,1)} %param.23) | copy-start | bytes 3076
  63.5 8.4 %copy-start.7 = (f32[1,2,512]{2,1,0:T(2,128)S(1)}, f32[1,2,512]{2,1,0:T(2,128)}, u32[]{:S(2)}) copy-start(f32[1,2,512]{2,1,0:T(2,128)} %param.21) | copy-start | bytes 12292
  63.6 71.0 %copy-start.5 = (bf16[128,512]{1,0:T(8,128)(2,1)S(1)}, bf16[128,512]{1,0:T(8,128)(2,1)}, u32[]{:S(2)}) copy-start(bf16[128,512]{1,0:T(8,128)(2,1)} %param.16) | copy-start | bytes 393220
  68.2 51.6 %all-to-all-start.1 = ((bf16[32,256,128]{2,1,0:T(8,128)(2,1)}), bf16[32,256,128]{2,1,0:T(8,128)(2,1)S(1)}, u32[]{:S(2)}, u32[]{:S(2)}) async-start(bf16[32,256,128]{2,1,0:T(8,128)(2,1)} %select_select_fusion), calls=%async_computation.1 | async-start | bytes 4194304 | tf_op jit(solution)/shard_map/all_to_all | solution.py:105
  138.3 3.4 copy-start.1
  139.3 2.6 copy-start.10
  218.0 101.8 %copy-start.4 = (bf16[1,512,512]{2,1,0:T(8,128)(2,1)S(1)}, bf16[1,512,512]{2,1,0:T(8,128)(2,1)}, u32[]{:S(2)}) copy-start(bf16[1,512,512]{2,1,0:T(8,128)(2,1)} %param.18) | copy-start | bytes 1572868
  326.9 3.2 copy-start.2
  326.9 4.2 %copy-start.11 = (bf16[1,512,1024]{2,1,0:T(8,128)(2,1)S(1)}, bf16[1,512,1024]{2,1,0:T(8,128)(2,1)}, u32[]{:S(2)}) copy-start(bf16[1,512,1024]{2,1,0:T(8,128)(2,1)} %param.19) | copy-start | bytes 3145732
  347.0 5.8 %copy-start.3 = (f32[4096,512]{0,1:T(8,128)S(1)}, f32[4096,512]{0,1:T(8,128)}, u32[]{:S(2)}) copy-start(f32[4096,512]{0,1:T(8,128)} %get-tuple-element.76) | copy-start | bytes 25165828
  347.0 5.8 %copy-start.6 = (f32[512]{0:T(512)S(1)}, f32[512]{0:T(512)}, u32[]{:S(2)}) copy-start(f32[512]{0:T(512)} %convert_element_type.67) | copy-start | bytes 6148
  347.0 5.8 %copy-start.8 = (f32[512]{0:T(512)S(1)}, f32[512]{0:T(512)}, u32[]{:S(2)}) copy-start(f32[512]{0:T(512)} %param.22) | copy-start | bytes 6148
where the time goes:
time: 358 us; the launch traced here: 356 us
  local copies, waits for them, and re-layouts  140 us (39%)
  matrix products  133 us (37%)
  waiting for transfers between devices  47.8 us (13%)
  other arithmetic  17.4 us (5%)
  blocking collectives  13.7 us (4%)
    sub x8, matrix products, attend_slate(): probs = jax.nn.softmax(scores, axis=-1).astype(jnp.bfloat16)  57.8 us
    all_to_all x1, waiting for transfers between devices, per_device(): lax.all_to_all(found, ('gx', 'gy'), split_axis=0, concat_axis=0, tiled=True)  47.8 us
    dot_general x8, matrix products, attend_slate(): jnp.einsum('hqk,khd->qhd', probs, values, preferred_element_type=jnp.floa...  35.3 us
    gather x1, local copies, waits for them, and re-layouts, fetch_rows(): rows = jnp.take(item_table, jnp.maximum(flat, 0), axis=0)  31.2 us
    while x3, local copies, waits for them, and re-layouts, score_slates(): lax.map(attend_slate, (query, keys, values)).reshape(slates * length, model)  29.2 us
    dot_general x1, matrix products, score_slates(): jnp.dot(inner, w_down[0], preferred_element_type=jnp.float32)  15.8 us
    scatter x1, local copies, waits for them, and re-layouts, per_device(): jnp.full((shards * capacity,), -1, jnp.int32).at[position].set(row_index)  15.5 us
    gather x1, local copies, waits for them, and re-layouts, per_device(): emb = jnp.take(returned, position, axis=0).reshape(slates, length, width)  14.9 us
  transfers between devices with their start and end apart: 1, of which 1 were waited for; matrix products, arithmetic and copies ran while one was open for 0% of the time, Pallas kernels for 0%

commit v1 on v0

v1 whole, which is shorter than its diff:
```python
import functools
import jax
import jax.numpy as jnp
from jax import lax
from jax.experimental import pallas as pl
from jax.experimental.pallas import tpu as pltpu
from jax.sharding import PartitionSpec as P

HEADS = 8
PICK = 32
CHUNKS = 2
LOG2E = 1.4426950408889634


def layer_norm(values, gain):
    mean = jnp.mean(values, axis=-1, keepdims=True)
    centred = values - mean
    variance = jnp.mean(centred * centred, axis=-1, keepdims=True)
    return centred * lax.rsqrt(variance + 1e-05) * gain


def slate_kernel(chunks, place_ref, *refs):
    returned_refs = refs[:chunks]
    (
        w_in_ref, w_qkv_ref, w_out_ref, w_up_ref, w_down_ref, gains_ref, fgain_ref, score_ref,
        out_ref, rows_ref, emb_ref,
    ) = refs[chunks:]
    f32, bf16 = jnp.float32, jnp.bfloat16
    slate = pl.program_id(0)

    @pl.when(slate == 0)
    def _():
        for chunk, ref in enumerate(returned_refs):
            size = ref.shape[0]
            rows_ref[chunk * size : (chunk + 1) * size, :] = ref[...].astype(f32)

    base = slate * emb_ref.shape[0]

    def pick(block, carry):
        for row in range(PICK):
            index = block * PICK + row
            emb_ref[pl.ds(index, 1), :] = rows_ref[pl.ds(place_ref[base + index], 1), :]
        return carry

    lax.fori_loop(0, emb_ref.shape[0] // PICK, pick, 0)
    model = w_in_ref.shape[1]
    head_dim = model // HEADS
    length = emb_ref.shape[0]
    pack = 128 // head_dim
    resid = jnp.dot(emb_ref[...].astype(bf16), w_in_ref[...], preferred_element_type=f32)
    normed = layer_norm(resid, gains_ref[0:1, :]).astype(bf16)
    query = jnp.dot(normed, w_qkv_ref[:, :model], preferred_element_type=f32)
    query = (query * (LOG2E * head_dim ** (-0.5))).astype(bf16)
    keys = jnp.dot(normed, w_qkv_ref[:, model : 2 * model], preferred_element_type=f32).astype(bf16)
    values = jnp.dot(normed, w_qkv_ref[:, 2 * model :], preferred_element_type=f32).astype(bf16)
    ones = jnp.ones((length, 128), bf16)
    lane = lax.broadcasted_iota(jnp.int32, (length, 128), 1) // head_dim
    mixed = []
    for group in range(HEADS // pack):
        cols = slice(group * 128, (group + 1) * 128)
        q_g, k_g = query[:, cols], keys[:, cols]
        v_g = jnp.concatenate([values[:, cols], ones], axis=1)
        total = None
        for part in range(pack):
            q_h = jnp.where(lane == part, q_g, jnp.zeros_like(q_g))
            scores = lax.dot_general(q_h, k_g, (((1,), (1,)), ((), ())), preferred_element_type=f32)
            top = jnp.max(scores, axis=-1, keepdims=True)
            probs = jnp.exp2(scores - top).astype(bf16)
            both = jnp.dot(probs, v_g, preferred_element_type=f32)
            head = both[:, :128] / both[:, 128:]
            total = head if total is None else jnp.where(lane == part, head, total)
        mixed.append(total.astype(bf16))
    mixed = jnp.concatenate(mixed, axis=1)
    resid = resid + jnp.dot(mixed, w_out_ref[...], preferred_element_type=f32)
    normed = layer_norm(resid, gains_ref[1:2, :]).astype(bf16)
    inner = jax.nn.gelu(jnp.dot(normed, w_up_ref[...], preferred_element_type=f32)).astype(bf16)
    resid = resid + jnp.dot(inner, w_down_ref[...], preferred_element_type=f32)
    terms = layer_norm(resid, fgain_ref[...]) * score_ref[...]
    folded = terms[:, :128]
    for start in range(128, model, 128):
        folded = folded + terms[:, start : start + 128]
    logits = jnp.sum(folded.T, axis=0, keepdims=True)
    shifted = logits - jnp.max(logits, axis=-1, keepdims=True)
    out_ref[0] = shifted - jnp.log(jnp.sum(jnp.exp(shifted), axis=-1, keepdims=True))


def score_slates(returned, position, w_in, w_qkv, w_out, w_up, w_down, norm_gains, final_gain, w_score):
    slates, length = position.shape
    chunks, width = len(returned), returned[0].shape[1]
    weights = (
        w_in,
        w_qkv[0],
        w_out[0],
        w_up[0],
        w_down[0],
        norm_gains[0],
        final_gain[None, :],
        w_score.astype(jnp.float32)[None, :],
    )
    whole = lambda w: pl.BlockSpec(w.shape, lambda s, place: (0, 0))
    out = pl.pallas_call(
        functools.partial(slate_kernel, chunks),
        grid_spec=pltpu.PrefetchScalarGridSpec(
            num_scalar_prefetch=1,
            grid=(slates,),
            in_specs=[whole(w) for w in (*returned, *weights)],
            out_specs=pl.BlockSpec((1, 1, length), lambda s, place: (s, 0, 0)),
            scratch_shapes=[
                pltpu.VMEM((chunks * returned[0].shape[0], width), jnp.float32),
                pltpu.VMEM((length, width), jnp.float32),
            ],
        ),
        out_shape=jax.ShapeDtypeStruct((slates, 1, length), jnp.float32),
        compiler_params=pltpu.CompilerParams(vmem_limit_bytes=60 * 1024 * 1024),
        name="slates",
    )(position.reshape(-1), *returned, *weights)
    return out.reshape(slates, length)


def slots_and_requests(owner, row_index, shards, capacity, length):
    total = owner.shape[0]
    onehot = (owner[:, None] == jnp.arange(shards, dtype=jnp.int32)[None, :]).astype(jnp.bfloat16)
    blocks = onehot.reshape(total // length, length, shards)
    lower = (jnp.arange(length)[:, None] >= jnp.arange(length)[None, :]).astype(jnp.bfloat16)
    within = jnp.einsum("ij,bjn->bin", lower, blocks, preferred_element_type=jnp.float32)
    totals = within[:, -1, :]
    before = jnp.cumsum(totals, axis=0) - totals
    counts = within + before[:, None, :]
    picked = jnp.sum(counts * blocks.astype(jnp.float32), axis=-1)
    slot = (picked.reshape(total) - 1.0).astype(jnp.int32)
    at_slot = (slot[:, None] == jnp.arange(capacity, dtype=jnp.int32)[None, :]).astype(jnp.bfloat16)
    digits = jnp.stack([row_index >> 16, (row_index >> 8) & 255, row_index & 255], axis=1).astype(jnp.bfloat16)
    placed = (onehot[:, None, :] * digits[:, :, None]).reshape(total, 3 * shards)
    found = lax.dot_general(placed, at_slot, (((0,), (0,)), ((), ())), preferred_element_type=jnp.float32)
    found = found.astype(jnp.int32).reshape(3, shards, capacity)
    return slot, (found[0] << 16) + (found[1] << 8) + found[2]


def exchange_kernel(blocks_ref, out_ref, send_sems, recv_sems, own_sem):
    inner = lax.axis_size("gy")
    count = lax.axis_size("gx") * inner
    here = lax.axis_index("gx") * inner + lax.axis_index("gy")
    barrier = pltpu.get_barrier_semaphore()

    def place(step):
        peer = lax.rem(here + step, count)
        return peer, (peer // inner, lax.rem(peer, inner))

    def copy_of(step):
        peer, device = place(step)
        return pltpu.make_async_remote_copy(
            src_ref=blocks_ref.at[peer],
            dst_ref=out_ref.at[here],
            send_sem=send_sems.at[step],
            recv_sem=recv_sems.at[step],
            device_id=device,
            device_id_type=pl.DeviceIdType.MESH,
        )

    @pl.loop(1, count)
    def _(step):
        pl.semaphore_signal(barrier, inc=1, device_id=place(step)[1], device_id_type=pl.DeviceIdType.MESH)

    own = pltpu.make_async_copy(blocks_ref.at[here], out_ref.at[here], own_sem)
    own.start()
    pl.semaphore_wait(barrier, count - 1)

    @pl.loop(1, count)
    def _(step):
        copy_of(step).start()

    @pl.loop(1, count)
    def _(step):
        copy_of(step).wait()

    own.wait()


def exchange(blocks, collective_id, space):
    count = blocks.shape[0]
    return pl.pallas_call(
        exchange_kernel,
        out_shape=jax.ShapeDtypeStruct(blocks.shape, blocks.dtype),
        in_specs=[pl.BlockSpec(memory_space=space)],
        out_specs=pl.BlockSpec(memory_space=space),
        scratch_shapes=[
            pltpu.SemaphoreType.DMA((count,)),
            pltpu.SemaphoreType.DMA((count,)),
            pltpu.SemaphoreType.DMA,
        ],
        compiler_params=pltpu.CompilerParams(
            collective_id=collective_id, has_side_effects=True, vmem_limit_bytes=32 * 1024 * 1024
        ),
        name="exchange",
    )(blocks)


def pick_kernel(asked_ref, table_ref, out_ref, rows_ref, stage_ref):
    step, steps = pl.program_id(0), pl.num_programs(0)
    size = table_ref.shape[0]
    start = pl.multiple_of(step * size, size)
    rows_ref[pl.ds(start, size), :] = table_ref[...].astype(jnp.float32)

    @pl.when(step == steps - 1)
    def _():
        def pick(block, carry):
            for row in range(PICK):
                index = block * PICK + row
                stage_ref[pl.ds(index, 1), :] = rows_ref[pl.ds(asked_ref[index], 1), :]
            return carry

        lax.fori_loop(0, out_ref.shape[0] // PICK, pick, 0)
        out_ref[...] = stage_ref[...].astype(out_ref.dtype)


def pick_rows(item_table, asked):
    rows, width = item_table.shape
    count = asked.shape[0]
    size = next(size for size in range(4608, 0, -16) if rows % size == 0)
    return pl.pallas_call(
        pick_kernel,
        grid_spec=pltpu.PrefetchScalarGridSpec(
            num_scalar_prefetch=1,
            grid=(rows // size,),
            in_specs=[pl.BlockSpec((size, width), lambda s, asked: (s, 0))],
            out_specs=pl.BlockSpec((count, width), lambda s, asked: (0, 0)),
            scratch_shapes=[pltpu.VMEM((rows, width), jnp.float32), pltpu.VMEM((count, width), jnp.float32)],
        ),
        out_shape=jax.ShapeDtypeStruct((count, width), item_table.dtype),
        compiler_params=pltpu.CompilerParams(vmem_limit_bytes=60 * 1024 * 1024),
        name="pick_rows",
    )(asked, item_table)


def per_device(
    candidate_owner,
    candidate_row,
    item_table,
    w_in,
    w_qkv,
    w_out,
    w_up,
    w_down,
    norm_gains,
    final_gain,
    w_score,
):
    slates, length, unused = candidate_owner.shape
    width = item_table.shape[1]
    shards = lax.axis_size(("gx", "gy"))
    capacity = max(2, 2 * slates * length // shards)
    owner = candidate_owner.reshape(slates * length)
    row_index = candidate_row.reshape(slates * length)
    slot, outgoing = slots_and_requests(owner, row_index, shards, capacity, length)
    wanted = exchange(outgoing[:, None, :], 0, pltpu.VMEM).reshape(shards, capacity)
    chunks = CHUNKS if capacity % CHUNKS == 0 else 1
    depth = capacity // chunks
    returned = []
    for chunk in range(chunks):
        asked = wanted[:, chunk * depth : (chunk + 1) * depth].reshape(-1)
        found = pick_rows(item_table, asked).reshape(shards, depth, width)
        back = lax.all_to_all(found, ("gx", "gy"), split_axis=0, concat_axis=0, tiled=True)
        returned.append(back.reshape(shards * depth, width))
    position = (slot // depth) * (shards * depth) + owner * depth + slot % depth
    position = position.reshape(slates, length)
    return score_slates(
        returned, position, w_in, w_qkv, w_out, w_up, w_down, norm_gains, final_gain, w_score
    )


def solution(mesh):
    return jax.shard_map(
        per_device,
        mesh=mesh,
        in_specs=(
            P(("gx", "gy"), None, None),
            P(("gx", "gy"), None),
            P(("gx", "gy"), None),
            P(),
            P(),
            P(),
            P(),
            P(),
            P(),
            P(),
            P(),
        ),
        out_specs=P(("gx", "gy"), None),
        check_vma=False,
    )
```

time: 358 us -> 159 us (0.44)
  local copies, waits for them, and re-layouts: 140 us -> 3.77 us
  matrix products: 133 us -> 1.26 us
  Pallas kernels: 0 us -> 109 us
  waiting for transfers between devices: 47.8 us -> 32 us
  other arithmetic: 17.4 us -> 3.26 us
  blocking collectives: 13.7 us -> 0 us
  starting transfers between devices: 3.11 us -> 8.19 us
    pallas_call x0 -> x4, Pallas kernels: none -> 109 us  [the longest x1 60.4 us: score_slates(): pl.pallas_call(functools.partial(slate_kernel, chunks), grid_spec=pltpu.P...]
    dot_general x15 -> x2, matrix products: 75.4 us -> 1.26 us  [the longest x1 0.91 us: slots_and_requests(): lax.dot_general(placed, at_slot, (((0,), (0,)), ((), ())), preferred_elem...]
    sub x8 -> x0, matrix products: 57.8 us -> none  [attend_slate(): probs = jax.nn.softmax(scores, axis=-1).astype(jnp.bfloat16)]
    gather x2 -> x0, local copies, waits for them, and re-layouts: 46.1 us -> none  [the longest x1 31.2 us: fetch_rows(): rows = jnp.take(item_table, jnp.maximum(flat, 0), axis=0)]
    reshape x4 -> x1, local copies, waits for them, and re-layouts: 33.6 us -> 0.61 us  [per_device(): asked = wanted[:, chunk * depth:(chunk + 1) * depth].reshape(-1)]
    while x3 -> x0, local copies, waits for them, and re-layouts: 29.2 us -> none  [score_slates(): lax.map(attend_slate, (query, keys, values)).reshape(slates * length, model)]
    all_to_all x1 -> x2, waiting for transfers between devices: 47.8 us -> 32 us  [per_device(): lax.all_to_all(found, ('gx', 'gy'), split_axis=0, concat_axis=0, tiled=True)]
    scatter x1 -> x0, local copies, waits for them, and re-layouts: 15.5 us -> none  [per_device(): jnp.full((shards * capacity,), -1, jnp.int32).at[position].set(row_index)]
  transfers between devices with their start and end apart: 1 -> 2, of which waited for: 1 -> 2; matrix products, arithmetic and copies ran while one was open for 0% -> 1% of each run, Pallas kernels for 0% -> 12%
where the time goes in v1:
time: 159 us; the launch traced here: 158 us
  Pallas kernels  109 us (69%)
  waiting for transfers between devices  32 us (20%)
  starting transfers between devices  8.19 us (5%)
  local copies, waits for them, and re-layouts  3.77 us (2%)
  other arithmetic  3.26 us (2%)
    pallas_call x1, Pallas kernels, score_slates(): pl.pallas_call(functools.partial(slate_kernel, chunks), grid_spec=pltpu.P...  60.4 us
    pallas_call x2, Pallas kernels, pick_rows(): pl.pallas_call(pick_kernel, grid_spec=pltpu.PrefetchScalarGridSpec(num_sc...  38.6 us
    all_to_all x2, waiting for transfers between devices, per_device(): lax.all_to_all(found, ('gx', 'gy'), split_axis=0, concat_axis=0, tiled=True)  32 us
    pallas_call x1, Pallas kernels, exchange(): pl.pallas_call(exchange_kernel, out_shape=jax.ShapeDtypeStruct(blocks.sha...  10.2 us
    all_to_all x2, starting transfers between devices, per_device(): lax.all_to_all(found, ('gx', 'gy'), split_axis=0, concat_axis=0, tiled=True)  8.19 us
  transfers between devices with their start and end apart: 2, of which 2 were waited for; matrix products, arithmetic and copies ran while one was open for 1% of the time, Pallas kernels for 12%

profile of v1, /device:TPU:1, one launch (start us, length us, event | category | flops | bytes accessed | tf_op | source)
XLA Modules:
  0.0 157.8 jit_solution(10334667758274662063)
XLA Ops:
  0.0 0.7 fusion.17
  0.8 0.7 copy.25
  1.5 0.8 fusion.6
  2.3 0.3 convolution_bitcast_fusion
  2.6 0.2 fusion.20
  2.8 0.2 multiply_reduce_fusion
  3.1 0.1 pad_maximum_fusion
  3.1 0.1 broadcast_multiply_fusion
  3.2 0.9 fusion.2
  4.2 10.2 %exchange.1 = s32[32,1,256]{2,1,0:T(1,128)S(1)} custom-call(s32[32,1,256]{2,1,0:T(1,128)S(1)} %add.49.blocks_ref), custom_call_target="tpu_custom_call" | custom-call | tf_op jit(solution)/shard_map/exchange/pallas_call | solution.py:181
  14.4 0.6 slice_bitcast_fusion
  15.0 19.2 %pick_rows.2 = bf16[4096,128]{1,0:T(8,128)(2,1)} custom-call(s32[4096]{0:T(1024)} %get-tuple-element.6.asked_ref, bf16[78336,128]{1,0:T(8,128)(2,1)} %table_ref.3), custom_call_target="tpu_custom_call" | custom-call | tf_op jit(solution)/shard_map/pick_rows/pallas_call | solution.py:220
  34.2 5.0 %all-to-all-start = ((bf16[32,128,128]{2,1,0:T(8,128)(2,1)}), bf16[32,128,128]{2,1,0:T(8,128)(2,1)S(1)}, u32[]{:S(2)}, u32[]{:S(2)}) async-start(bf16[32,128,128]{2,1,0:T(8,128)(2,1)} %bitcast.53), calls=%async_computation | async-start | bytes 2097152 | tf_op jit(solution)/shard_map/all_to_all | solution.py:262
  39.2 0.0 copy-start.3
  39.3 0.0 copy-start.2
  39.3 19.4 %pick_rows.3 = bf16[4096,128]{1,0:T(8,128)(2,1)} custom-call(s32[4096]{0:T(1024)} %get-tuple-element.5.asked_ref, bf16[78336,128]{1,0:T(8,128)(2,1)} %table_ref.3), custom_call_target="tpu_custom_call" | custom-call | tf_op jit(solution)/shard_map/pick_rows/pallas_call | solution.py:220
  58.7 6.9 %all-to-all-done = bf16[32,128,128]{2,1,0:T(8,128)(2,1)S(1)} async-done(((bf16[32,128,128]{2,1,0:T(8,128)(2,1)}), bf16[32,128,128]{2,1,0:T(8,128)(2,1)S(1)}, u32[]{:S(2)}, u32[]{:S(2)}) %all-to-all-start) | async-done | bytes 1048608 | tf_op jit(solution)/shard_map/all_to_all | solution.py:262
  65.6 0.0 copy-start
  65.6 3.2 %all-to-all-start.1 = ((bf16[32,128,128]{2,1,0:T(8,128)(2,1)}), bf16[32,128,128]{2,1,0:T(8,128)(2,1)S(1)}, u32[]{:S(2)}, u32[]{:S(2)}) async-start(bf16[32,128,128]{2,1,0:T(8,128)(2,1)} %bitcast.51), calls=%async_computation.1 | async-start | bytes 2097152 | tf_op jit(solution)/shard_map/all_to_all | solution.py:262
  68.7 0.0 copy-done.3
  68.7 0.6 broadcast_in_dim.9
  69.3 0.0 copy-done.2
  69.3 0.6 fusion.12.place_ref
  70.0 25.1 %all-to-all-done.1 = bf16[32,128,128]{2,1,0:T(8,128)(2,1)S(1)} async-done(((bf16[32,128,128]{2,1,0:T(8,128)(2,1)}), bf16[32,128,128]{2,1,0:T(8,128)(2,1)S(1)}, u32[]{:S(2)}, u32[]{:S(2)}) %all-to-all-start.1) | async-done | bytes 1048608 | tf_op jit(solution)/shard_map/all_to_all | solution.py:262
  95.1 0.0 copy-start.1
  95.1 0.0 copy-done
  95.1 1.0 copy-done.1
  96.1 60.4 %slates.1 = f32[8,1,512]{2,1,0:T(1,128)} custom-call(s32[4096]{0:T(1024)} %fusion.12.place_ref, bf16[4096,128]{1,0:T(8,128)(2,1)} %bitcast.50, bf16[4096,128]{1,0:T(8,128)(2,1)} %bitcast.52, bf16[128,512]{1,0:T(8,128)(2,1)} %refs_2_.1, bf16[512,1536]{1,0:T(8,128)(2,1)} %bitcast.54, bf16[512,512]{1,0:T(8,128)(2,1)} %bitcast.58, bf16[512,1024]{1,0:T(8,128)(2,1)} %bitcast.55, ...), custom_call_target="tpu_custom_call" | custom-call | tf_op jit(solution)/shard_map/slates/pallas_call | solution.py:101
  156.5 1.3 copy.24
  (8 shorter events, 0.1 us)
Async XLA Ops:
  34.2 31.4 %all-to-all-start = ((bf16[32,128,128]{2,1,0:T(8,128)(2,1)}), bf16[32,128,128]{2,1,0:T(8,128)(2,1)S(1)}, u32[]{:S(2)}, u32[]{:S(2)}) async-start(bf16[32,128,128]{2,1,0:T(8,128)(2,1)} %bitcast.53), calls=%async_computation | async-start | bytes 2097152 | tf_op jit(solution)/shard_map/all_to_all | solution.py:262
  39.2 29.5 %copy-start.3 = (bf16[512]{0:T(512)(128)(2,1)S(1)}, bf16[512]{0:T(512)(128)(2,1)}, u32[]{:S(2)}) copy-start(bf16[512]{0:T(512)(128)(2,1)} %param.21) | copy-start | bytes 3076
  39.3 30.1 %copy-start.2 = (s32[8,512,1]{1,2,0:T(1,128)S(1)}, s32[8,512,1]{1,2,0:T(1,128)}, u32[]{:S(2)}) copy-start(s32[8,512,1]{1,2,0:T(1,128)} %param.11) | copy-start | bytes 49156
  65.6 29.5 %copy-start = (bf16[32,128,128]{2,1,0:T(8,128)(2,1)}, bf16[32,128,128]{2,1,0:T(8,128)(2,1)S(1)}, u32[]{:S(2)}) copy-start(bf16[32,128,128]{2,1,0:T(8,128)(2,1)S(1)} %all-to-all-done) | copy-start | bytes 3145732
  65.6 29.5 %all-to-all-start.1 = ((bf16[32,128,128]{2,1,0:T(8,128)(2,1)}), bf16[32,128,128]{2,1,0:T(8,128)(2,1)S(1)}, u32[]{:S(2)}, u32[]{:S(2)}) async-start(bf16[32,128,128]{2,1,0:T(8,128)(2,1)} %bitcast.51), calls=%async_computation.1 | async-start | bytes 2097152 | tf_op jit(solution)/shard_map/all_to_all | solution.py:262
  95.1 1.0 copy-start.1
